TPU v7x, 32 devices: a whole 2x2x4 slice. The times are simulated.
32 devices in a mesh: row: 2 (over core), sa: 16 (over z, y, x).
Axes of the slice: x: 2, y: 2, z: 4, core: 2. Of those that a mesh axis runs over, the one named last changes fastest.
Arguments:
- rep_w1: float32 [4, 2, 64, 4096], P('row', None, None, 'sa'), may hold values from -6 to 6
- rep_w3: float32 [4, 2, 64, 4096], P('row', None, None, 'sa'), may hold values from -6 to 6
- rep_w2: float32 [4, 2, 64, 4096], P('row', None, None, 'sa'), may hold values from -6 to 6
- rep_gate: float32 [4, 2, 4096], P('row', None, 'sa'), may hold values from -6 to 6
Outputs:
- serve_w1: bfloat16 [2, 64, 4096], P('row', 'sa')
- serve_w3: bfloat16 [2, 64, 4096], P('row', 'sa')
- serve_w2: bfloat16 [2, 64, 4096], P('row', 'sa')
- serve_gate: bfloat16 [2, 4096], replicated
- soup_norms: float32 [2, 4], P('row')
- replica_norms: float32 [4, 2, 4], P('row')
All inputs are finite; a program needn't handle non-finite values.
Results may differ from a plain program's by a relative error of at most 0.001.
Values may be sent and summed in bfloat16 or wider, within the bound.
A program may use at most 64 MiB of HBM per device.

v0:
```python
import jax
import jax.numpy as jnp
from jax import lax
from jax.sharding import PartitionSpec as P


def own_rows_2(product, width, axis):
    everything = product(jnp.int32(0), lax.axis_size(axis) * width)
    own = lax.psum_scatter(everything, axis, scatter_dimension=0, tiled=True)
    return own


def square_sums(values, dims_summed):
    return jnp.sum(values * values, axis=dims_summed)


def local(rep_w1, rep_w3, rep_w2, rep_gate):
    rows_total = lax.axis_size("row")
    replicas = rep_w1.shape[0] * rows_total
    experts_all = rep_w1.shape[1]
    expert_rows = experts_all // rows_total
    hidden_all = rep_w1.shape[2]
    model_width = rep_w1.shape[3] * lax.axis_size("sa")
    weights = (rep_w1, rep_w3, rep_w2)
    replica_parts = jnp.stack(
        [square_sums(weight, (2, 3)) for weight in weights] + [square_sums(rep_gate, 2)], axis=2
    )

    def expert_terms(offset, length):
        pieces = [
            jnp.sum(lax.dynamic_slice_in_dim(weight, offset, length, 1), axis=0)
            for weight in weights
        ]
        return jnp.stack(pieces, axis=1)

    summed = own_rows_2(expert_terms, expert_rows, "row")
    served = (summed / replicas).astype(jnp.bfloat16)
    arranged = lax.all_to_all(served, "sa", split_axis=2, concat_axis=3, tiled=True)
    served_list = [arranged[:, column] for column in range(3)]
    gate_local = jnp.sum(rep_gate, axis=0)
    gate_total = lax.psum(gate_local, "row")
    gate_shard = (gate_total / replicas).astype(jnp.bfloat16)
    serve_gate = lax.all_gather(gate_shard, "sa", axis=1, tiled=True)
    own_rows = lax.dynamic_slice_in_dim(
        gate_shard, lax.axis_index("row") * expert_rows, expert_rows, 0
    )
    soup_parts = jnp.stack(
        [square_sums(served.astype(jnp.float32), (1, 2)) for served in served_list]
        + [square_sums(own_rows.astype(jnp.float32), 1)],
        axis=1,
    )
    replica_total, soup_total = lax.psum((replica_parts, soup_parts), "sa")
    counts = jnp.array([hidden_all * model_width] * 3 + [model_width], jnp.float32)
    replica_norms = jnp.sqrt(replica_total / counts)
    soup_norms = jnp.sqrt(soup_total / counts)
    return (served_list[0], served_list[1], served_list[2], serve_gate, soup_norms, replica_norms)


def solution(mesh):
    placed = (
        P("row", None, None, "sa"),
        P("row", None, None, "sa"),
        P("row", None, None, "sa"),
        P("row", None, "sa"),
    )
    return jax.shard_map(
        local,
        mesh=mesh,
        in_specs=placed,
        out_specs=(
            P("row", "sa", None),
            P("row", "sa", None),
            P("row", "sa", None),
            P(),
            P("row", None),
            P("row", None, None),
        ),
        check_vma=False,
    )
```

profile of v0, /device:TPU:0, one launch (start us, length us, event | category | flops | bytes accessed | tf_op | source)
XLA Modules:
  0.0 122.1 jit_solution(15603964799628544858)
XLA Ops:
  7.2 0.0 reduce-scatter.2.cloned.1.call-start
  7.2 1.1 multiply_reduce_fusion.2
  8.3 1.1 multiply_reduce_fusion
  9.5 0.8 copy.15
  10.3 0.0 reduce-scatter.2.cloned.1.call-update
  10.3 0.7 copy-done.1
  11.0 0.1 multiply_reduce_fusion.6
  11.0 2.6 %psum.21 = f32[2,256]{1,0:T(2,128)S(1)} all-reduce(f32[2,256]{1,0:T(2,128)S(1)} %get-tuple-element.37), channel_id=1, replica_groups=mesh['row'=2,'sa'=16] {'row'}, use_global_device_ids=true, to_apply=%region_5.0 | all-reduce | flops 512 | bytes 4096 | tf_op jit(solution)/shard_map/psum | solution.py:41
  13.7 7.4 %reduce-scatter.2.cloned.1.call-done = f32[1,3,64,256]{3,2,1,0:T(8,128)} async-done(((f32[2,3,64,256]{3,2,1,0:T(8,128)}), f32[1,3,64,256]{3,2,1,0:T(8,128)}) %reduce-scatter.2.cloned.1.call-update) | async-done | bytes 196624 | tf_op jit(solution)/shard_map/reduce_scatter | solution.py:9
  21.0 0.9 multiply_convert_fusion
  21.9 0.7 copy.16
  22.7 6.7 %all-to-all-start = ((bf16[1,3,64,256]{3,1,0,2:T(4,128)(2,1)}), bf16[1,3,64,256]{3,1,0,2:T(4,128)(2,1)S(1)}, u32[]{:S(2)}, u32[]{:S(2)}) async-start(bf16[1,3,64,256]{3,1,0,2:T(4,128)(2,1)} %copy.16), calls=%async_computation.1 | async-start | bytes 262144 | tf_op jit(solution)/shard_map/all_to_all | solution.py:38
  29.4 0.6 multiply_reduce_fusion.7
  30.0 41.0 %all_gather.3 = bf16[2,4096]{1,0:T(2,128)(2,1)S(1)} all-gather(bf16[2,256]{1,0:T(2,128)(2,1)S(1)} %multiply_convert_fusion.1), channel_id=1, replica_groups=mesh['row'=2,'sa'=16] {'sa'}, dimensions={1}, use_global_device_ids=true | all-gather | bytes 17408 | tf_op jit(solution)/shard_map/all_gather | solution.py:43
  71.1 1.3 %multiply_reduce_fusion.3 = (f32[]{:T(128)}, bf16[1,4,4096]{2,1,0:T(4,128)(2,1)}, f32[]{:T(128)}, bf16[1,4,4096]{2,1,0:T(4,128)(2,1)}, f32[]{:T(128)}, /*index=5*/bf16[1,4,4096]{2,1,0:T(4,128)(2,1)}) fusion(bf16[1,3,4,4096]{3,2,1,0:T(4,128)(2,1)S(1)} %bitcast.28), kind=kLoop, calls=%fused_computation.5 | loop fusion | flops 147453 | bytes 196620 | tf_op jit(solution)/shard_map/reduce_sum | solution.py:14
  72.4 2.6 %pad_maximum_fusion.2 = f32[1,4]{1,0:T(1,128)S(1)} fusion(f32[1,1]{1,0:T(1,128)} %bitcast.13, f32[1,1]{1,0:T(1,128)} %bitcast.12, f32[1,1]{1,0:T(1,128)} %bitcast.11, f32[1,1]{1,0:T(1,128)} %bitcast.10), kind=kLoop, calls=%fused_computation.16 | loop fusion | flops 12 | bytes 32 | tf_op jit(solution)/shard_map/stack | solution.py:47
  75.0 37.0 %all-reduce = (f32[1,4]{1,0:T(1,128)S(1)}, f32[2,2,4]{1,0,2:T(2,128)S(1)}) all-reduce(f32[1,4]{1,0:T(1,128)S(1)} %pad_maximum_fusion.2, f32[2,2,4]{1,0,2:T(2,128)S(1)} %pad_maximum_fusion.1), channel_id=1, replica_groups=mesh['row'=2,'sa'=16] {'sa'}, use_global_device_ids=true, to_apply=%region_10.0 | all-reduce | flops 20 | bytes 160 | tf_op jit(solution)/shard_map/psum | solution.py:52
  112.0 0.0 copy-start.2
  112.0 0.6 copy-done.2
  112.7 0.1 multiply_sqrt_fusion
  112.8 0.7 copy.18
  113.4 0.7 copy-done.3
  114.1 0.5 multiply_sqrt_fusion.1
  114.6 0.6 copy.21
  (9 shorter events, 0.1 us)
Async XLA Ops:
  7.2 1.2 copy-start
  7.2 13.8 %reduce-scatter.2.cloned.1.call-start = ((), (), s32[]{:S(2)}) async-start(), calls=%async_computation.2 | async-start | bytes 589824 | tf_op jit(solution)/shard_map/reduce_scatter | solution.py:9
  10.3 0.7 copy-start.1
  22.7 48.4 %all-to-all-start = ((bf16[1,3,64,256]{3,1,0,2:T(4,128)(2,1)}), bf16[1,3,64,256]{3,1,0,2:T(4,128)(2,1)S(1)}, u32[]{:S(2)}, u32[]{:S(2)}) async-start(bf16[1,3,64,256]{3,1,0,2:T(4,128)(2,1)} %copy.16), calls=%async_computation.1 | async-start | bytes 262144 | tf_op jit(solution)/shard_map/all_to_all | solution.py:38
  112.0 0.7 copy-start.2
  113.4 0.7 copy-start.3
Sparse Core Ops, SparseCore 0:
  10.4 10.5 reduce-scatter.1
where the time goes:
time: 122 us
  blocking collectives  80.7 us (66%)
  between operations  14.1 us (12%)
  other arithmetic  8.38 us (7%)
  waiting for transfers between devices  7.37 us (6%)
  starting transfers between devices  6.75 us (6%)
  local copies, waits for them, and re-layouts  4.79 us (4%)
    all_gather x1, blocking collectives, local(): serve_gate = lax.all_gather(gate_shard, 'sa', axis=1, tiled=True)  41 us
    psum x1, blocking collectives, local(): replica_total, soup_total = lax.psum((replica_parts, soup_parts), 'sa')  37 us
    reduce_scatter x1, waiting for transfers between devices, own_rows_2(): own = lax.psum_scatter(everything, axis, scatter_dimension=0, tiled=True)  7.35 us
    all_to_all x1, starting transfers between devices, local(): lax.all_to_all(served, 'sa', split_axis=2, concat_axis=3, tiled=True)  6.72 us
    reduce_sum x5, other arithmetic, square_sums(): return jnp.sum(values * values, axis=dims_summed)  4.24 us
    unnamed x10, local copies, waits for them, and re-layouts  3.25 us
    psum x1, blocking collectives, local(): gate_total = lax.psum(gate_local, 'row')  2.6 us
    another operation x1, other arithmetic, local(): jnp.stack([square_sums(served.astype(jnp.float32), (1, 2)) for served in...  2.57 us
  transfers between devices with their start and end apart: 2, of which 1 were waited for; matrix products, arithmetic and copies ran while one was open for 1% of the time, Pallas kernels for 0%

commit v1 on v0

--- a/solution.py
+++ b/solution.py
@@ -40,7 +40,7 @@
     gate_local = jnp.sum(rep_gate, axis=0)
     gate_total = lax.psum(gate_local, "row")
     gate_shard = (gate_total / replicas).astype(jnp.bfloat16)
-    serve_gate = lax.all_gather(gate_shard, "sa", axis=1, tiled=True)
+    serve_gate = jnp.concatenate(lax.all_gather(gate_shard, "sa"), axis=1)
     own_rows = lax.dynamic_slice_in_dim(
         gate_shard, lax.axis_index("row") * expert_rows, expert_rows, 0
     )

time: 122 us -> 122 us (level)
  no operation moved by 1% of the time
where the time goes in v1:
time: 122 us
  blocking collectives  80.7 us (66%)
  between operations  14.1 us (12%)
  other arithmetic  8.39 us (7%)
  waiting for transfers between devices  7.37 us (6%)
  starting transfers between devices  6.75 us (6%)
  local copies, waits for them, and re-layouts  4.79 us (4%)
    all_gather x1, blocking collectives, local(): serve_gate = jnp.concatenate(lax.all_gather(gate_shard, 'sa'), axis=1)  41 us
    psum x1, blocking collectives, local(): replica_total, soup_total = lax.psum((replica_parts, soup_parts), 'sa')  37 us
    reduce_scatter x1, waiting for transfers between devices, own_rows_2(): own = lax.psum_scatter(everything, axis, scatter_dimension=0, tiled=True)  7.35 us
    all_to_all x1, starting transfers between devices, local(): lax.all_to_all(served, 'sa', split_axis=2, concat_axis=3, tiled=True)  6.72 us
    reduce_sum x5, other arithmetic, square_sums(): return jnp.sum(values * values, axis=dims_summed)  4.24 us
    unnamed x10, local copies, waits for them, and re-layouts  3.25 us
    psum x1, blocking collectives, local(): gate_total = lax.psum(gate_local, 'row')  2.6 us
    another operation x1, other arithmetic, local(): jnp.stack([square_sums(served.astype(jnp.float32), (1, 2)) for served in...  2.57 us
  transfers between devices with their start and end apart: 2, of which 1 were waited for; matrix products, arithmetic and copies ran while one was open for 1% of the time, Pallas kernels for 0%

profile of v1, /device:TPU:0, one launch (start us, length us, event | category | flops | bytes accessed | tf_op | source)
XLA Modules:
  0.0 122.1 jit_solution(10588655764540912956)
XLA Ops:
  7.2 0.0 reduce-scatter.2.cloned.1.call-start
  7.2 1.1 multiply_reduce_fusion.2
  8.3 1.1 multiply_reduce_fusion
  9.5 0.8 copy.15
  10.3 0.0 reduce-scatter.2.cloned.1.call-update
  10.3 0.7 copy-done.1
  11.0 0.1 multiply_reduce_fusion.6
  11.0 2.6 %psum.21 = f32[2,256]{1,0:T(2,128)S(1)} all-reduce(f32[2,256]{1,0:T(2,128)S(1)} %get-tuple-element.37), channel_id=1, replica_groups=mesh['row'=2,'sa'=16] {'row'}, use_global_device_ids=true, to_apply=%region_5.0 | all-reduce | flops 512 | bytes 4096 | tf_op jit(solution)/shard_map/psum | solution.py:41
  13.7 7.3 %reduce-scatter.2.cloned.1.call-done = f32[1,3,64,256]{3,2,1,0:T(8,128)} async-done(((f32[2,3,64,256]{3,2,1,0:T(8,128)}), f32[1,3,64,256]{3,2,1,0:T(8,128)}) %reduce-scatter.2.cloned.1.call-update) | async-done | bytes 196624 | tf_op jit(solution)/shard_map/reduce_scatter | solution.py:9
  21.0 0.9 multiply_convert_fusion
  21.9 0.7 copy.16
  22.7 6.7 %all-to-all-start = ((bf16[1,3,64,256]{3,1,0,2:T(4,128)(2,1)}), bf16[1,3,64,256]{3,1,0,2:T(4,128)(2,1)S(1)}, u32[]{:S(2)}, u32[]{:S(2)}) async-start(bf16[1,3,64,256]{3,1,0,2:T(4,128)(2,1)} %copy.16), calls=%async_computation.1 | async-start | bytes 262144 | tf_op jit(solution)/shard_map/all_to_all | solution.py:38
  29.4 0.6 multiply_reduce_fusion.7
  30.0 41.0 %all-gather.1 = bf16[16,2,256]{2,1,0:T(2,128)(2,1)S(1)} all-gather(bf16[1,2,256]{2,1,0:T(2,128)(2,1)S(1)} %fusion), channel_id=2, replica_groups=mesh['row'=2,'sa'=16] {'sa'}, dimensions={0}, use_global_device_ids=true | all-gather | bytes 17408 | tf_op jit(solution)/shard_map/all_gather | solution.py:43
  71.1 1.3 %multiply_reduce_fusion.3 = (f32[]{:T(128)}, bf16[1,4,4096]{2,1,0:T(4,128)(2,1)}, f32[]{:T(128)}, bf16[1,4,4096]{2,1,0:T(4,128)(2,1)}, f32[]{:T(128)}, /*index=5*/bf16[1,4,4096]{2,1,0:T(4,128)(2,1)}) fusion(bf16[1,3,4,4096]{3,2,1,0:T(4,128)(2,1)S(1)} %bitcast.33), kind=kLoop, calls=%fused_computation.5 | loop fusion | flops 147453 | bytes 196620 | tf_op jit(solution)/shard_map/reduce_sum | solution.py:14
  72.4 2.6 %pad_maximum_fusion.2 = f32[1,4]{1,0:T(1,128)S(1)} fusion(f32[1,1]{1,0:T(1,128)} %bitcast.16, f32[1,1]{1,0:T(1,128)} %bitcast.15, f32[1,1]{1,0:T(1,128)} %bitcast.14, f32[1,1]{1,0:T(1,128)} %bitcast.13), kind=kLoop, calls=%fused_computation.16 | loop fusion | flops 12 | bytes 32 | tf_op jit(solution)/shard_map/stack | solution.py:47
  75.0 37.0 %all-reduce = (f32[1,4]{1,0:T(1,128)S(1)}, f32[2,2,4]{1,0,2:T(2,128)S(1)}) all-reduce(f32[1,4]{1,0:T(1,128)S(1)} %pad_maximum_fusion.2, f32[2,2,4]{1,0,2:T(2,128)S(1)} %pad_maximum_fusion.1), channel_id=1, replica_groups=mesh['row'=2,'sa'=16] {'sa'}, use_global_device_ids=true, to_apply=%region_10.0 | all-reduce | flops 20 | bytes 160 | tf_op jit(solution)/shard_map/psum | solution.py:52
  112.0 0.0 copy-start.2
  112.0 0.6 copy-done.2
  112.7 0.1 multiply_sqrt_fusion
  112.8 0.7 copy.18
  113.4 0.7 copy-done.3
  114.1 0.5 multiply_sqrt_fusion.1
  114.6 0.6 copy.21
  (10 shorter events, 0.1 us)
Async XLA Ops:
  7.2 1.2 copy-start
  7.2 13.8 %reduce-scatter.2.cloned.1.call-start = ((), (), s32[]{:S(2)}) async-start(), calls=%async_computation.2 | async-start | bytes 589824 | tf_op jit(solution)/shard_map/reduce_scatter | solution.py:9
  10.3 0.7 copy-start.1
  22.7 48.4 %all-to-all-start = ((bf16[1,3,64,256]{3,1,0,2:T(4,128)(2,1)}), bf16[1,3,64,256]{3,1,0,2:T(4,128)(2,1)S(1)}, u32[]{:S(2)}, u32[]{:S(2)}) async-start(bf16[1,3,64,256]{3,1,0,2:T(4,128)(2,1)} %copy.16), calls=%async_computation.1 | async-start | bytes 262144 | tf_op jit(solution)/shard_map/all_to_all | solution.py:38
  112.0 0.7 copy-start.2
  113.4 0.7 copy-start.3
Sparse Core Ops, SparseCore 0:
  10.4 10.5 reduce-scatter.1
